TPU v7x, 32 devices: a whole 2x2x4 slice. The times are simulated.
32 devices in a mesh: seq: 8 (over y, x, core), head: 4 (over z).
Axes of the slice: x: 2, y: 2, z: 4, core: 2. Of those that a mesh axis runs over, the one named last changes fastest.
Arguments:
- tokens: bfloat16 [32, 1024, 1024], P('seq'), may hold values from -6 to 6
- w_query: bfloat16 [1024, 1024], P(None, 'head'), may hold values from -1 to 1
- w_key: bfloat16 [1024, 1024], P(None, 'head'), may hold values from -1 to 1
- w_value: bfloat16 [1024, 1024], P(None, 'head'), may hold values from -0.1875 to 0.1875
- w_out: bfloat16 [1024, 1024], P('head'), may hold values from -0.1875 to 0.1875
Outputs:
- mixed: bfloat16 [32, 1024, 1024], P('seq', None, 'head')
All inputs are finite; a program needn't handle non-finite values.
Results may differ from a plain program's by a relative error of at most 0.012.
Values may be sent and summed in bfloat16 or wider, within the bound.
No kernel may reach another device: no remote copies, remote signals or barrier semaphores. Data moves between devices by JAX's collectives and lax.ppermute only.
A program may use at most 128 MiB of HBM per device.

v0:
```python
import jax
import jax.numpy as jnp
from jax import lax
from jax.sharding import PartitionSpec as P

HS = 64
epsilon = 1e-05


def normalize(tokens):
    values = tokens.astype(jnp.float32)
    row_mean = jnp.mean(values, axis=-1, keepdims=True)
    centered = values - row_mean
    row_var = jnp.mean(centered * centered, axis=-1, keepdims=True)
    return (centered * lax.rsqrt(row_var + epsilon)).astype(jnp.bfloat16)


def project(source, weight):
    return jnp.einsum("fpd,dc->fpc", source, weight, preferred_element_type=jnp.float32).astype(
        jnp.bfloat16
    )


def attend(queries, key_rows, value_rows, head_count):
    frames, patch_count, feature_width = queries.shape
    head_size = feature_width // head_count
    query_flat = queries.reshape(frames, patch_count * head_count, head_size)
    key_flat = key_rows.reshape(frames, patch_count * head_count, head_size)
    value_flat = value_rows.reshape(frames, patch_count * head_count, head_size)
    scores = jnp.einsum(
        "fmd,gmd->fgm", query_flat, key_flat, preferred_element_type=jnp.float32
    ) * head_size ** (-0.5)
    row_top = jnp.max(scores, axis=1, keepdims=True)
    raised = jnp.exp(scores - row_top)
    weights = (raised / jnp.sum(raised, axis=1, keepdims=True)).astype(jnp.bfloat16)
    attended = jnp.einsum("fgm,gmd->fmd", weights, value_flat, preferred_element_type=jnp.float32)
    return attended.astype(jnp.bfloat16).reshape(frames, patch_count, feature_width)


def local(tokens, w_query, w_key, w_value, w_out):
    normed = normalize(tokens)
    head_count = w_query.shape[1] // HS
    local_query = project(normed, w_query)
    local_key = project(normed, w_key)
    local_value = project(normed, w_value)
    queries, key_rows, value_rows = (
        lax.all_to_all(local_query, "seq", split_axis=1, concat_axis=0, tiled=True),
        lax.all_to_all(local_key, "seq", split_axis=1, concat_axis=0, tiled=True),
        lax.all_to_all(local_value, "seq", split_axis=1, concat_axis=0, tiled=True),
    )
    attended = attend(queries, key_rows, value_rows, head_count)
    partial_value = jnp.einsum("fpc,cd->fpd", attended, w_out, preferred_element_type=jnp.float32)
    columns = lax.psum_scatter(
        partial_value.astype(jnp.bfloat16), "head", scatter_dimension=2, tiled=True
    )
    return lax.all_to_all(columns, "seq", split_axis=0, concat_axis=1, tiled=True)


def solution(mesh):
    return jax.shard_map(
        local,
        mesh=mesh,
        in_specs=(
            P("seq", None, None),
            P(None, "head"),
            P(None, "head"),
            P(None, "head"),
            P("head", None),
        ),
        out_specs=P("seq", None, "head"),
        check_vma=False,
    )
```

profile of v0, /device:TPU:0, one launch (start us, length us, event | category | flops | bytes accessed | tf_op | source)
XLA Modules:
  0.0 326.3 jit_solution(13314724638309537397)
XLA Ops:
  6.5 0.0 copy-start
  6.5 0.0 copy-start.1
  6.5 0.0 copy-start.3
  6.5 4.7 %convert_reduce_fusion = f32[4,1024]{1,0:T(4,128)S(1)} fusion(bf16[4,1024,1024]{2,1,0:T(8,128)(2,1)} %param.5), kind=kLoop, calls=%fused_computation.2 | loop fusion | flops 8384512 | bytes 8404992 | tf_op jit(solution)/shard_map/reduce_sum | solution.py:12
  11.3 1.1 copy-done.1
  12.4 2.8 fusion.3
  15.2 0.0 copy-done.3
  15.2 3.1 fusion.28
  18.3 0.0 copy-start.4
  18.4 3.0 copy.19
  21.3 5.2 %all-to-all-start.1 = ((bf16[4,1024,256]{2,0,1:T(4,128)(2,1)}), bf16[4,1024,256]{2,0,1:T(4,128)(2,1)S(1)}, u32[]{:S(2)}, u32[]{:S(2)}) async-start(bf16[4,1024,256]{2,0,1:T(4,128)(2,1)} %copy.19), calls=%async_computation.1 | async-start | bytes 4194304 | tf_op jit(solution)/shard_map/all_to_all | solution.py:48
  26.5 0.0 copy-done.4
  26.5 5.0 %fusion.31 = bf16[4,1024,256]{2,1,0:T(8,128)(2,1)S(1)} fusion(bf16[4,1024,1024]{2,1,0:T(8,128)(2,1)} %param.5, f32[4,1024]{1,0:T(4,128)S(1)} %add_rsqrt_fusion, f32[4,1024]{1,0:T(4,128)S(1)} %broadcast_multiply_fusion, bf16[1024,256]{1,0:T(8,128)(2,1)S(1)} %copy-done.4), kind=kOutput, calls=%fused_computation.30 | convolution fusion | flops 2165309440 | bytes 11042816 | tf_op jit(solution)/shard_map/fpd,dc->fpc/dot_general | solution.py:19
  31.5 0.0 copy-start.5
  31.6 2.9 copy.21
  34.5 18.6 %all-to-all-done.1 = bf16[4,1024,256]{2,0,1:T(4,128)(2,1)S(1)} async-done(((bf16[4,1024,256]{2,0,1:T(4,128)(2,1)}), bf16[4,1024,256]{2,0,1:T(4,128)(2,1)S(1)}, u32[]{:S(2)}, u32[]{:S(2)}) %all-to-all-start.1) | async-done | bytes 2097184 | tf_op jit(solution)/shard_map/all_to_all | solution.py:48
  53.1 0.0 copy-start.2
  53.1 4.3 %all-to-all-start.2 = ((bf16[4,1024,256]{2,0,1:T(4,128)(2,1)}), bf16[4,1024,256]{2,0,1:T(4,128)(2,1)}, u32[]{:S(2)}, u32[]{:S(2)}) async-start(bf16[4,1024,256]{2,0,1:T(4,128)(2,1)} %copy.21), calls=%async_computation.2 | async-start | bytes 4194304 | tf_op jit(solution)/shard_map/all_to_all | solution.py:47
  57.5 0.0 copy-done.5
  57.5 5.0 %fusion.25 = bf16[4,1024,256]{2,1,0:T(8,128)(2,1)S(1)} fusion(bf16[4,1024,1024]{2,1,0:T(8,128)(2,1)} %param.5, f32[4,1024]{1,0:T(4,128)S(1)} %add_rsqrt_fusion, f32[4,1024]{1,0:T(4,128)S(1)} %broadcast_multiply_fusion, bf16[1024,256]{1,0:T(8,128)(2,1)S(1)} %copy-done.5), kind=kOutput, calls=%fused_computation.28 | convolution fusion | flops 2165309440 | bytes 11042816 | tf_op jit(solution)/shard_map/fpd,dc->fpc/dot_general | solution.py:19
  62.5 0.0 copy-done.2
  62.5 2.9 copy.17
  65.5 18.7 %all-to-all-done.2 = bf16[4,1024,256]{2,0,1:T(4,128)(2,1)} async-done(((bf16[4,1024,256]{2,0,1:T(4,128)(2,1)}), bf16[4,1024,256]{2,0,1:T(4,128)(2,1)}, u32[]{:S(2)}, u32[]{:S(2)}) %all-to-all-start.2) | async-done | bytes 2097184 | tf_op jit(solution)/shard_map/all_to_all | solution.py:47
  84.1 4.4 %all-to-all-start = ((bf16[4,1024,256]{2,0,1:T(4,128)(2,1)}), bf16[4,1024,256]{2,0,1:T(4,128)(2,1)}, u32[]{:S(2)}, u32[]{:S(2)}) async-start(bf16[4,1024,256]{2,0,1:T(4,128)(2,1)} %copy.17), calls=%async_computation | async-start | bytes 4194304 | tf_op jit(solution)/shard_map/all_to_all | solution.py:49
  88.5 0.2 reduce-scatter.2.cloned.1.call-start
  88.7 2.0 copy.42
  90.7 3.3 reshape.30
  94.0 2.0 copy.41
  95.9 3.2 reshape.31
  99.2 8.3 %fusion.18 = f32[512,32,32]{2,1,0:T(8,128)S(1)} fusion(bf16[32,512,64]{2,1,0:T(8,128)(2,1)} %reshape.31, bf16[32,512,64]{2,1,0:T(8,128)(2,1)} %reshape.30), kind=kOutput, calls=%fused_computation.19 | convolution fusion | flops 67108864 | bytes 6291456 | tf_op jit(solution)/shard_map/fmd,gmd->fgm/dot_general | solution.py:30
  107.5 6.1 %fusion.39 = (f32[32,512]{0,1:T(8,128)S(1)}, f32[32,32,512]{0,1,2:T(8,128)}) fusion(f32[512,32,32]{2,1,0:T(8,128)S(1)} %fusion.18), kind=kOutput, calls=%fused_computation.38 | output fusion | flops 2097183 | bytes 4259840 | tf_op jit(solution)/shard_map/sub | solution.py:34
  113.6 1.5 all-to-all-done
  115.1 2.0 copy.43
  117.1 3.3 %reshape.29 = bf16[32,512,64]{2,1,0:T(8,128)(2,1)} reshape(bf16[8,4,128,256]{3,2,1,0:T(8,128)(2,1)S(1)} %bitcast.50) | data formatting | bytes 4194304 | tf_op jit(solution)/shard_map/reshape | solution.py:29
  120.4 8.1 %convert_bitcast_fusion = bf16[32,512,64]{2,0,1:T(8,128)(2,1)S(1)} fusion(f32[32,32,512]{0,1,2:T(8,128)} %get-tuple-element.6, f32[32,512]{0,1:T(8,128)S(1)} %get-tuple-element.5, bf16[32,512,64]{2,1,0:T(8,128)(2,1)} %reshape.29), kind=kOutput, calls=%fused_computation.22 | convolution fusion | flops 69206016 | bytes 6356992 | tf_op jit(solution)/shard_map/fgm,gmd->fmd/dot_general | solution.py:36
  128.5 3.6 %copy.27 = bf16[32,512,64]{2,1,0:T(8,128)(2,1)} copy(bf16[32,512,64]{2,0,1:T(8,128)(2,1)S(1)} %convert_bitcast_fusion) | data formatting | bytes 4194304 | tf_op jit(solution)/shard_map/convert_element_type | solution.py:37
  132.1 5.5 %reshape.32 = bf16[32,128,256]{2,1,0:T(8,128)(2,1)S(1)} reshape(bf16[32,512,64]{2,1,0:T(8,128)(2,1)} %copy.27) | data formatting | bytes 4194304 | tf_op jit(solution)/shard_map/reshape | solution.py:37
  137.6 0.0 copy-done
  137.6 5.6 %convolution_convert_fusion = bf16[32,128,1024]{2,1,0:T(8,128)(2,1)} fusion(bf16[32,128,256]{2,1,0:T(8,128)(2,1)S(1)} %reshape.32, bf16[256,1024]{1,0:T(8,128)(2,1)S(1)} %copy-done), kind=kOutput, calls=%fused_computation.13 | convolution fusion | flops 2151677952 | bytes 11010048 | tf_op jit(solution)/shard_map/fpc,cd->fpd/dot_general | solution.py:52
  143.1 0.0 reduce-scatter.2.cloned.1.call-update
  143.2 144.7 %reduce-scatter.2.cloned.1.call-done = bf16[32,128,256]{2,1,0:T(8,128)(2,1)} async-done(((bf16[32,128,1024]{2,1,0:T(8,128)(2,1)}), bf16[32,128,256]{2,1,0:T(8,128)(2,1)}) %reduce-scatter.2.cloned.1.call-update) | async-done | bytes 2097168 | tf_op jit(solution)/shard_map/reduce_scatter | solution.py:53
  287.8 30.2 %all_to_all.63 = bf16[32,128,256]{2,1,0:T(8,128)(2,1)S(1)} all-to-all(bf16[32,128,256]{2,1,0:T(8,128)(2,1)} %reduce-scatter.2.cloned.1.call-done), channel_id=1, replica_groups=mesh['seq'=8,'head'=4] {'seq'}, dimensions={0} | all-to-all | bytes 4194304 | tf_op jit(solution)/shard_map/all_to_all | solution.py:56
  318.0 1.5 copy.28
  (2 shorter events, 0.0 us)
Async XLA Ops:
  6.5 131.0 %copy-start = (bf16[256,1024]{1,0:T(8,128)(2,1)S(1)}, bf16[256,1024]{1,0:T(8,128)(2,1)}, u32[]{:S(2)}) copy-start(bf16[256,1024]{1,0:T(8,128)(2,1)} %param.9) | copy-start | bytes 1572868
  6.5 5.8 %copy-start.1 = (bf16[4,1024,1024]{2,1,0:T(8,128)(2,1)S(1)}, bf16[4,1024,1024]{2,1,0:T(8,128)(2,1)}, u32[]{:S(2)}) copy-start(bf16[4,1024,1024]{2,1,0:T(8,128)(2,1)} %param.5) | copy-start | bytes 25165828
  6.5 8.6 %copy-start.3 = (bf16[1024,256]{1,0:T(8,128)(2,1)S(1)}, bf16[1024,256]{1,0:T(8,128)(2,1)}, u32[]{:S(2)}) copy-start(bf16[1024,256]{1,0:T(8,128)(2,1)} %param.7) | copy-start | bytes 1572868
  18.3 8.2 %copy-start.4 = (bf16[1024,256]{1,0:T(8,128)(2,1)S(1)}, bf16[1024,256]{1,0:T(8,128)(2,1)}, u32[]{:S(2)}) copy-start(bf16[1024,256]{1,0:T(8,128)(2,1)} %param.6) | copy-start | bytes 1572868
  21.3 31.8 %all-to-all-start.1 = ((bf16[4,1024,256]{2,0,1:T(4,128)(2,1)}), bf16[4,1024,256]{2,0,1:T(4,128)(2,1)S(1)}, u32[]{:S(2)}, u32[]{:S(2)}) async-start(bf16[4,1024,256]{2,0,1:T(4,128)(2,1)} %copy.19), calls=%async_computation.1 | async-start | bytes 4194304 | tf_op jit(solution)/shard_map/all_to_all | solution.py:48
  31.5 25.9 %copy-start.5 = (bf16[1024,256]{1,0:T(8,128)(2,1)S(1)}, bf16[1024,256]{1,0:T(8,128)(2,1)}, u32[]{:S(2)}) copy-start(bf16[1024,256]{1,0:T(8,128)(2,1)} %param.8) | copy-start | bytes 1572868
  53.1 9.4 %copy-start.2 = (bf16[4,1024,256]{2,0,1:T(4,128)(2,1)}, bf16[4,1024,256]{2,0,1:T(4,128)(2,1)S(1)}, u32[]{:S(2)}) copy-start(bf16[4,1024,256]{2,0,1:T(4,128)(2,1)S(1)} %all-to-all-done.1) | copy-start | bytes 6291460
  53.1 31.0 %all-to-all-start.2 = ((bf16[4,1024,256]{2,0,1:T(4,128)(2,1)}), bf16[4,1024,256]{2,0,1:T(4,128)(2,1)}, u32[]{:S(2)}, u32[]{:S(2)}) async-start(bf16[4,1024,256]{2,0,1:T(4,128)(2,1)} %copy.21), calls=%async_computation.2 | async-start | bytes 4194304 | tf_op jit(solution)/shard_map/all_to_all | solution.py:47
  84.1 31.0 %all-to-all-start = ((bf16[4,1024,256]{2,0,1:T(4,128)(2,1)}), bf16[4,1024,256]{2,0,1:T(4,128)(2,1)}, u32[]{:S(2)}, u32[]{:S(2)}) async-start(bf16[4,1024,256]{2,0,1:T(4,128)(2,1)} %copy.17), calls=%async_computation | async-start | bytes 4194304 | tf_op jit(solution)/shard_map/all_to_all | solution.py:49
  88.5 199.3 %reduce-scatter.2.cloned.1.call-start = ((), (), s32[]{:S(2)}) async-start(), calls=%async_computation.5 | async-start | bytes 10485760 | tf_op jit(solution)/shard_map/reduce_scatter | solution.py:53
Sparse Core Ops, SparseCore 0:
  143.3 144.4 reduce-scatter.1
where the time goes:
time: 327 us; the launch traced here: 326 us
  waiting for transfers between devices  184 us (56%)
  local copies, waits for them, and re-layouts  36.1 us (11%)
  matrix products  35.2 us (11%)
  blocking collectives  30.2 us (9%)
  starting transfers between devices  14.1 us (4%)
  other arithmetic  13.6 us (4%)
  between operations  13.6 us (4%)
    reduce_scatter x1, waiting for transfers between devices, local(): lax.psum_scatter(partial_value.astype(jnp.bfloat16), 'head', scatter_dime...  145 us
    all_to_all x1, blocking collectives, local(): lax.all_to_all(columns, 'seq', split_axis=0, concat_axis=1, tiled=True)  30.2 us
    all_to_all x1, waiting for transfers between devices, local(): lax.all_to_all(local_query, 'seq', split_axis=1, concat_axis=0, tiled=True)  18.7 us
    all_to_all x1, waiting for transfers between devices, local(): lax.all_to_all(local_key, 'seq', split_axis=1, concat_axis=0, tiled=True)  18.6 us
    dot_general x3, matrix products, project(): jnp.einsum('fpd,dc->fpc', source, weight, preferred_element_type=jnp.floa...  13.2 us
    convert_element_type x3, local copies, waits for them, and re-layouts, project(): jnp.einsum('fpd,dc->fpc', source, weight, preferred_element_type=jnp.floa...  8.83 us
    dot_general x1, matrix products, attend(): jnp.einsum('fmd,gmd->fgm', query_flat, key_flat, preferred_element_type=j...  8.29 us
    dot_general x1, matrix products, attend(): jnp.einsum('fgm,gmd->fmd', weights, value_flat, preferred_element_type=jn...  8.14 us
  transfers between devices with their start and end apart: 4, of which 4 were waited for; matrix products, arithmetic and copies ran while one was open for 12% of the time, Pallas kernels for 0%

commit v1 on v0

--- a/solution.py
+++ b/solution.py
@@ -38,13 +38,21 @@
 
 
 def local(tokens, w_query, w_key, w_value, w_out):
+
+    def fit_sheets(slab_in):
+        arr_out = jnp.concatenate(
+            lax.all_to_all(jnp.stack(jnp.split(slab_in, lax.axis_size("seq"), 1), 0), "seq", 0, 0),
+            0,
+        )
+        return arr_out
+
     normed = normalize(tokens)
     head_count = w_query.shape[1] // HS
     local_query = project(normed, w_query)
     local_key = project(normed, w_key)
     local_value = project(normed, w_value)
     queries, key_rows, value_rows = (
-        lax.all_to_all(local_query, "seq", split_axis=1, concat_axis=0, tiled=True),
+        fit_sheets(local_query),
         lax.all_to_all(local_key, "seq", split_axis=1, concat_axis=0, tiled=True),
         lax.all_to_all(local_value, "seq", split_axis=1, concat_axis=0, tiled=True),
     )

time: 327 us -> 332 us (1.015)
  local copies, waits for them, and re-layouts: 36.1 us -> 41.2 us
    unnamed x12 -> x17, local copies, waits for them, and re-layouts: 1.13 us -> 6.16 us
    another operation x0 -> x2, local copies, waits for them, and re-layouts: none -> 3.96 us  [the longest x1 3.24 us: attend(): query_flat = queries.reshape(frames, patch_count * head_count, head_size)]
    convert_element_type x3 -> x2, local copies, waits for them, and re-layouts: 8.83 us -> 5.94 us  [project(): jnp.einsum('fpd,dc->fpc', source, weight, preferred_element_type=jnp.floa...]
  transfers between devices with their start and end apart: 4 -> 4, of which waited for: 4 -> 3; matrix products, arithmetic and copies ran while one was open for 12% -> 13% of each run, Pallas kernels for 0% -> 0%
where the time goes in v1:
time: 332 us; the launch traced here: 331 us
  waiting for transfers between devices  183 us (55%)
  local copies, waits for them, and re-layouts  41.2 us (12%)
  matrix products  35.2 us (11%)
  blocking collectives  30.2 us (9%)
  starting transfers between devices  14.1 us (4%)
  other arithmetic  13.6 us (4%)
  between operations  13.5 us (4%)
    reduce_scatter x1, waiting for transfers between devices, local(): lax.psum_scatter(partial_value.astype(jnp.bfloat16), 'head', scatter_dime...  146 us
    all_to_all x1, blocking collectives, local(): lax.all_to_all(columns, 'seq', split_axis=0, concat_axis=1, tiled=True)  30.2 us
    all_to_all x1, waiting for transfers between devices, fit_sheets(): lax.all_to_all(jnp.stack(jnp.split(slab_in, lax.axis_size('seq'), 1), 0),...  18.6 us
    all_to_all x1, waiting for transfers between devices, local(): lax.all_to_all(local_key, 'seq', split_axis=1, concat_axis=0, tiled=True)  18.6 us
    dot_general x3, matrix products, project(): jnp.einsum('fpd,dc->fpc', source, weight, preferred_element_type=jnp.floa...  13.2 us
    dot_general x1, matrix products, attend(): jnp.einsum('fmd,gmd->fgm', query_flat, key_flat, preferred_element_type=j...  8.29 us
    dot_general x1, matrix products, attend(): jnp.einsum('fgm,gmd->fmd', weights, value_flat, preferred_element_type=jn...  8.14 us
  transfers between devices with their start and end apart: 4, of which 3 were waited for; matrix products, arithmetic and copies ran while one was open for 13% of the time, Pallas kernels for 0%

profile of v1, /device:TPU:0, one launch (start us, length us, event | category | flops | bytes accessed | tf_op | source)
XLA Modules:
  0.0 331.3 jit_solution(5498397499132221036)
XLA Ops:
  6.5 0.0 copy-start
  6.5 0.0 copy-start.1
  6.5 4.7 %convert_reduce_fusion = f32[4,1024]{1,0:T(4,128)S(1)} fusion(bf16[4,1024,1024]{2,1,0:T(8,128)(2,1)} %param.5), kind=kLoop, calls=%fused_computation.2 | loop fusion | flops 8384512 | bytes 8404992 | tf_op jit(solution)/shard_map/reduce_sum | solution.py:12
  11.3 1.1 copy-done.1
  12.4 0.0 copy-start.2
  12.4 2.8 fusion.3
  15.2 0.0 copy-done.2
  15.2 3.2 fusion.31
  18.4 0.0 copy-start.3
  18.4 0.7 fusion.45
  19.1 0.7 fusion.44
  19.8 0.7 fusion.43
  20.5 0.7 fusion.42
  21.2 0.7 fusion.41
  22.0 0.7 fusion.40
  22.7 0.7 fusion.39
  23.4 0.7 fusion.38
  24.1 5.2 %all-to-all-start.2 = ((bf16[8,4,128,256]{3,2,1,0:T(8,128)(2,1)}), bf16[8,4,128,256]{3,2,1,0:T(8,128)(2,1)S(1)}, u32[]{:S(2)}, u32[]{:S(2)}) async-start(bf16[8,4,128,256]{3,2,1,0:T(8,128)(2,1)} %fusion.38), calls=%async_computation.2 | async-start | bytes 4194304 | tf_op jit(solution)/shard_map/all_to_all | solution.py:44
  29.3 0.0 copy-done.3
  29.3 5.0 %fusion.28 = bf16[4,1024,256]{2,1,0:T(8,128)(2,1)S(1)} fusion(bf16[4,1024,1024]{2,1,0:T(8,128)(2,1)} %param.5, f32[4,1024]{1,0:T(4,128)S(1)} %add_rsqrt_fusion, f32[4,1024]{1,0:T(4,128)S(1)} %broadcast_multiply_fusion, bf16[1024,256]{1,0:T(8,128)(2,1)S(1)} %copy-done.3), kind=kOutput, calls=%fused_computation.28 | convolution fusion | flops 2165309440 | bytes 11042816 | tf_op jit(solution)/shard_map/fpd,dc->fpc/dot_general | solution.py:19
  34.3 0.0 copy-start.4
  34.4 2.9 copy.19
  37.3 18.6 %all-to-all-done.2 = bf16[8,4,128,256]{3,2,1,0:T(8,128)(2,1)S(1)} async-done(((bf16[8,4,128,256]{3,2,1,0:T(8,128)(2,1)}), bf16[8,4,128,256]{3,2,1,0:T(8,128)(2,1)S(1)}, u32[]{:S(2)}, u32[]{:S(2)}) %all-to-all-start.2) | async-done | bytes 2097184 | tf_op jit(solution)/shard_map/all_to_all | solution.py:44
  55.9 4.3 %all-to-all-start.1 = ((bf16[4,1024,256]{2,0,1:T(4,128)(2,1)}), bf16[4,1024,256]{2,0,1:T(4,128)(2,1)}, u32[]{:S(2)}, u32[]{:S(2)}) async-start(bf16[4,1024,256]{2,0,1:T(4,128)(2,1)} %copy.19), calls=%async_computation.1 | async-start | bytes 4194304 | tf_op jit(solution)/shard_map/all_to_all | solution.py:56
  60.3 0.0 copy-done.4
  60.3 5.0 %fusion.25 = bf16[4,1024,256]{2,1,0:T(8,128)(2,1)S(1)} fusion(bf16[4,1024,1024]{2,1,0:T(8,128)(2,1)} %param.5, f32[4,1024]{1,0:T(4,128)S(1)} %add_rsqrt_fusion, f32[4,1024]{1,0:T(4,128)S(1)} %broadcast_multiply_fusion, bf16[1024,256]{1,0:T(8,128)(2,1)S(1)} %copy-done.4), kind=kOutput, calls=%fused_computation.27 | convolution fusion | flops 2165309440 | bytes 11042816 | tf_op jit(solution)/shard_map/fpd,dc->fpc/dot_general | solution.py:19
  65.3 3.0 copy.17
  68.3 18.6 %all-to-all-done.1 = bf16[4,1024,256]{2,0,1:T(4,128)(2,1)} async-done(((bf16[4,1024,256]{2,0,1:T(4,128)(2,1)}), bf16[4,1024,256]{2,0,1:T(4,128)(2,1)}, u32[]{:S(2)}, u32[]{:S(2)}) %all-to-all-start.1) | async-done | bytes 2097184 | tf_op jit(solution)/shard_map/all_to_all | solution.py:56
  86.9 4.4 %all-to-all-start = ((bf16[4,1024,256]{2,0,1:T(4,128)(2,1)}), bf16[4,1024,256]{2,0,1:T(4,128)(2,1)}, u32[]{:S(2)}, u32[]{:S(2)}) async-start(bf16[4,1024,256]{2,0,1:T(4,128)(2,1)} %copy.17), calls=%async_computation | async-start | bytes 4194304 | tf_op jit(solution)/shard_map/all_to_all | solution.py:57
  91.3 0.2 reduce-scatter.2.cloned.1.call-start
  91.5 3.3 copy.38
  94.8 6.1 %reshape.26 = bf16[32,512,64]{2,1,0:T(8,128)(2,1)} reshape(bf16[8,4,128,256]{3,2,1,0:T(8,128)(2,1)} %bitcast.76) | data formatting | bytes 4194304 | tf_op jit(solution)/shard_map/reshape | solution.py:28
  100.9 3.2 reshape_reshape.3
  104.2 8.3 %fusion.18 = f32[512,32,32]{2,1,0:T(8,128)S(1)} fusion(bf16[32,512,64]{2,1,0:T(8,128)(2,1)} %reshape_reshape.3, bf16[32,512,64]{2,1,0:T(8,128)(2,1)} %reshape.26), kind=kOutput, calls=%fused_computation.19 | convolution fusion | flops 67108864 | bytes 6291456 | tf_op jit(solution)/shard_map/fmd,gmd->fgm/dot_general | solution.py:30
  112.5 6.1 %fusion.47 = (f32[32,512]{0,1:T(8,128)S(1)}, f32[32,32,512]{0,1,2:T(8,128)}) fusion(f32[512,32,32]{2,1,0:T(8,128)S(1)} %fusion.18), kind=kOutput, calls=%fused_computation.53 | output fusion | flops 2097183 | bytes 4259840 | tf_op jit(solution)/shard_map/sub | solution.py:34
  118.6 0.0 all-to-all-done
  118.6 2.0 copy.39
  120.6 3.3 reshape.25
  123.9 8.1 %convert_bitcast_fusion = bf16[32,512,64]{2,0,1:T(8,128)(2,1)S(1)} fusion(f32[32,32,512]{0,1,2:T(8,128)} %get-tuple-element.6, f32[32,512]{0,1:T(8,128)S(1)} %get-tuple-element.5, bf16[32,512,64]{2,1,0:T(8,128)(2,1)} %reshape.25), kind=kOutput, calls=%fused_computation.22 | convolution fusion | flops 69206016 | bytes 6356992 | tf_op jit(solution)/shard_map/fgm,gmd->fmd/dot_general | solution.py:36
  132.0 3.6 %copy.25 = bf16[32,512,64]{2,1,0:T(8,128)(2,1)} copy(bf16[32,512,64]{2,0,1:T(8,128)(2,1)S(1)} %convert_bitcast_fusion) | data formatting | bytes 4194304 | tf_op jit(solution)/shard_map/convert_element_type | solution.py:37
  135.6 5.5 %reshape.27 = bf16[32,128,256]{2,1,0:T(8,128)(2,1)S(1)} reshape(bf16[32,512,64]{2,1,0:T(8,128)(2,1)} %copy.25) | data formatting | bytes 4194304 | tf_op jit(solution)/shard_map/reshape | solution.py:37
  141.1 0.0 copy-done
  141.1 5.6 %convolution_convert_fusion = bf16[32,128,1024]{2,1,0:T(8,128)(2,1)} fusion(bf16[32,128,256]{2,1,0:T(8,128)(2,1)S(1)} %reshape.27, bf16[256,1024]{1,0:T(8,128)(2,1)S(1)} %copy-done), kind=kOutput, calls=%fused_computation.13 | convolution fusion | flops 2151677952 | bytes 11010048 | tf_op jit(solution)/shard_map/fpc,cd->fpd/dot_general | solution.py:60
  146.6 0.0 reduce-scatter.2.cloned.1.call-update
  146.7 146.2 %reduce-scatter.2.cloned.1.call-done = bf16[32,128,256]{2,1,0:T(8,128)(2,1)} async-done(((bf16[32,128,1024]{2,1,0:T(8,128)(2,1)}), bf16[32,128,256]{2,1,0:T(8,128)(2,1)}) %reduce-scatter.2.cloned.1.call-update) | async-done | bytes 2097168 | tf_op jit(solution)/shard_map/reduce_scatter | solution.py:61
  292.8 30.2 %all_to_all.53 = bf16[32,128,256]{2,1,0:T(8,128)(2,1)S(1)} all-to-all(bf16[32,128,256]{2,1,0:T(8,128)(2,1)} %reduce-scatter.2.cloned.1.call-done), channel_id=1, replica_groups=mesh['seq'=8,'head'=4] {'seq'}, dimensions={0} | all-to-all | bytes 4194304 | tf_op jit(solution)/shard_map/all_to_all | solution.py:64
  323.0 1.5 copy.26
  (2 shorter events, 0.0 us)
Async XLA Ops:
  6.5 134.5 %copy-start = (bf16[256,1024]{1,0:T(8,128)(2,1)S(1)}, bf16[256,1024]{1,0:T(8,128)(2,1)}, u32[]{:S(2)}) copy-start(bf16[256,1024]{1,0:T(8,128)(2,1)} %param.9) | copy-start | bytes 1572868
  6.5 5.8 %copy-start.1 = (bf16[4,1024,1024]{2,1,0:T(8,128)(2,1)S(1)}, bf16[4,1024,1024]{2,1,0:T(8,128)(2,1)}, u32[]{:S(2)}) copy-start(bf16[4,1024,1024]{2,1,0:T(8,128)(2,1)} %param.5) | copy-start | bytes 25165828
  12.4 2.8 copy-start.2
  18.4 11.0 %copy-start.3 = (bf16[1024,256]{1,0:T(8,128)(2,1)S(1)}, bf16[1024,256]{1,0:T(8,128)(2,1)}, u32[]{:S(2)}) copy-start(bf16[1024,256]{1,0:T(8,128)(2,1)} %param.7) | copy-start | bytes 1572868
  24.1 31.8 %all-to-all-start.2 = ((bf16[8,4,128,256]{3,2,1,0:T(8,128)(2,1)}), bf16[8,4,128,256]{3,2,1,0:T(8,128)(2,1)S(1)}, u32[]{:S(2)}, u32[]{:S(2)}) async-start(bf16[8,4,128,256]{3,2,1,0:T(8,128)(2,1)} %fusion.38), calls=%async_computation.2 | async-start | bytes 4194304 | tf_op jit(solution)/shard_map/all_to_all | solution.py:44
  34.3 25.9 %copy-start.4 = (bf16[1024,256]{1,0:T(8,128)(2,1)S(1)}, bf16[1024,256]{1,0:T(8,128)(2,1)}, u32[]{:S(2)}) copy-start(bf16[1024,256]{1,0:T(8,128)(2,1)} %param.8) | copy-start | bytes 1572868
  55.9 31.0 %all-to-all-start.1 = ((bf16[4,1024,256]{2,0,1:T(4,128)(2,1)}), bf16[4,1024,256]{2,0,1:T(4,128)(2,1)}, u32[]{:S(2)}, u32[]{:S(2)}) async-start(bf16[4,1024,256]{2,0,1:T(4,128)(2,1)} %copy.19), calls=%async_computation.1 | async-start | bytes 4194304 | tf_op jit(solution)/shard_map/all_to_all | solution.py:56
  86.9 31.7 %all-to-all-start = ((bf16[4,1024,256]{2,0,1:T(4,128)(2,1)}), bf16[4,1024,256]{2,0,1:T(4,128)(2,1)}, u32[]{:S(2)}, u32[]{:S(2)}) async-start(bf16[4,1024,256]{2,0,1:T(4,128)(2,1)} %copy.17), calls=%async_computation | async-start | bytes 4194304 | tf_op jit(solution)/shard_map/all_to_all | solution.py:57
  91.3 201.5 %reduce-scatter.2.cloned.1.call-start = ((), (), s32[]{:S(2)}) async-start(), calls=%async_computation.5 | async-start | bytes 10485760 | tf_op jit(solution)/shard_map/reduce_scatter | solution.py:61
Sparse Core Ops, SparseCore 0:
  146.8 146.0 reduce-scatter.1
